TPU v7x, 32 devices: a whole 2x2x4 slice. The times are simulated.
32 devices in a mesh: src: 16 (over z, y, x), hid: 2 (over core).
Axes of the slice: x: 2, y: 2, z: 4, core: 2. Of those that a mesh axis runs over, the one named last changes fastest.
Arguments:
- source_field: float32 [128, 2, 98, 128], P('src'), may hold values from -36 to 36
- hidden_gain: float32 [98], replicated, may hold values from 0.1 to 1.9
- enc_tiles: float32 [1024, 128, 128], P(('src', 'hid')), may hold values from -0.25 to 0.25
- enc_src_block: int32 [1024], P(('src', 'hid')), may hold values from 0 to 127, as said below
- enc_hid_block: int32 [1024], P(('src', 'hid')), may hold values from 0 to 63, as said below
- enc_count: int32 [32], P(('src', 'hid')), may hold values from 1 to 32, as said below
- dec_tiles: float32 [1024, 128, 128], P(('src', 'hid')), may hold values from -0.15625 to 0.15625
- dec_src_block: int32 [1024], P(('src', 'hid')), may hold values from 0 to 127, as said below
- dec_hid_block: int32 [1024], P(('src', 'hid')), may hold values from 0 to 63, as said below
- dec_count: int32 [32], P(('src', 'hid')), may hold values from 1 to 32, as said below
Outputs:
- returned: float32 [128, 2, 98, 128], P('src')
- channel_rms: float32 [98], replicated
Inputs may be any that keep to these rules, and one draw needn't show every extreme that they name: `enc_src_block`: the 32 entries starting at (s * 2 + h) * 32 lie in s * 8 to (s + 1) * 8 - 1. `enc_hid_block`: the 32 entries starting at (s * 2 + h) * 32 lie in h * 32 to (h + 1) * 32 - 1; within these entries no pair (enc_src_block, enc_hid_block) repeats. `enc_count`: entry s * 2 + h counts the live slots of that group; it equals 32 for some group. `dec_src_block`: the 32 entries starting at (s * 2 + h) * 32 lie in s * 8 to (s + 1) * 8 - 1. `dec_hid_block`: the 32 entries starting at (s * 2 + h) * 32 lie in h * 32 to (h + 1) * 32 - 1; within these entries no pair (dec_src_block, dec_hid_block) repeats. `dec_count`: entry s * 2 + h counts the live slots of that group; it equals 32 for some group.
All inputs are finite; a program needn't handle non-finite values.
Results may differ from a plain program's by a relative error of at most 0.0003.
Values sent between devices are 32-bit elements; how exact they have to be, the bound alone decides.
No kernel may reach another device: no remote copies, remote signals or barrier semaphores. Data moves between devices by JAX's collectives and lax.ppermute only.
A program may use at most 64 MiB of HBM per device.

v0:
```python
import jax
import jax.numpy as jnp
from jax import lax
from jax.sharding import PartitionSpec as P

HID_BLK = 32
GROUP = 16
HIGH = lax.Precision.HIGHEST
EPSILON = 1e-06


def normalize(total, gain, batch, channels):
    nodes, features, width = total.shape
    grouped = total.reshape(nodes, batch, channels, width)
    mean_square = jnp.mean(grouped * grouped, axis=2, keepdims=True)
    scaled = grouped * gain[None, None, :, None] * lax.rsqrt(mean_square + EPSILON)
    return scaled.reshape(nodes, features, width)


def body(
    source_field,
    hidden_gain,
    enc_tiles,
    enc_src_block,
    enc_hid_block,
    enc_count,
    dec_tiles,
    dec_src_block,
    dec_hid_block,
    dec_count,
):
    src_blocks, batch, channels, width = source_field.shape
    features = batch * channels
    flat = source_field.reshape(src_blocks, features, width)
    src_first = lax.axis_index("src") * src_blocks
    hid_first = lax.axis_index("hid") * HID_BLK
    enc_sources = enc_src_block - src_first
    enc_targets = enc_hid_block - hid_first
    dec_targets = dec_src_block - src_first
    dec_sources = dec_hid_block - hid_first
    src_range = jnp.arange(src_blocks, dtype=jnp.int32)
    hid_range = jnp.arange(HID_BLK, dtype=jnp.int32)
    slot_range = jnp.arange(GROUP, dtype=jnp.int32)

    def encode_group(step, partial_value):
        start = step * GROUP
        tiles = lax.dynamic_slice_in_dim(enc_tiles, start, GROUP, 0)
        sources = lax.dynamic_slice_in_dim(enc_sources, start, GROUP, 0)
        targets = lax.dynamic_slice_in_dim(enc_targets, start, GROUP, 0)
        alive = (start + slot_range < enc_count[0])[:, None]
        select = (sources[:, None] == src_range[None, :]).astype(jnp.float32)
        placing = (alive & (targets[:, None] == hid_range[None, :])).astype(jnp.float32)
        blocks = jnp.einsum("ts,sfc->tfc", select, flat, precision=HIGH)
        product = jnp.einsum("tfr,trc->tfc", blocks, tiles, precision=HIGH)
        return partial_value + jnp.einsum("th,tfc->hfc", placing, product, precision=HIGH)

    enc_groups = (enc_count[0] + GROUP - 1) // GROUP
    partial_value = lax.fori_loop(
        0, enc_groups, encode_group, jnp.zeros((HID_BLK, features, width), jnp.float32)
    )
    hidden = normalize(lax.psum(partial_value, "src"), hidden_gain, batch, channels)

    def fetch(start):
        sources = lax.dynamic_slice_in_dim(dec_sources, start, GROUP, 0)
        select = (sources[:, None] == hid_range[None, :]).astype(jnp.float32)
        return jnp.einsum("th,hfc->tfc", select, hidden, precision=HIGH)

    def decode_group(step, partial_back):
        start = step * GROUP
        tiles = lax.dynamic_slice_in_dim(dec_tiles, start, GROUP, 0)
        targets = lax.dynamic_slice_in_dim(dec_targets, start, GROUP, 0)
        alive = (start + slot_range < dec_count[0])[:, None]
        blocks = fetch(start)
        product = jnp.einsum("tfr,trc->tfc", blocks, tiles, precision=HIGH)
        placing = (alive & (targets[:, None] == src_range[None, :])).astype(jnp.float32)
        return partial_back + jnp.einsum("ts,tfc->sfc", placing, product, precision=HIGH)

    dec_groups = (dec_count[0] + GROUP - 1) // GROUP
    partial_back = lax.fori_loop(
        0, dec_groups, decode_group, jnp.zeros((src_blocks, features, width), jnp.float32)
    )
    total_points = src_blocks * lax.axis_size("src") * batch * width
    returned = lax.psum(partial_back, "hid")
    difference = returned - flat
    squares = jnp.sum(
        (difference * difference).reshape(src_blocks, batch, channels, width), axis=(0, 1, 3)
    )
    sums = lax.psum(squares, "src")
    channel_rms = jnp.sqrt(sums / total_points + EPSILON)
    return (returned.reshape(source_field.shape), channel_rms)


def solution(mesh):
    in_specs = (
        P("src", None, None, None),
        P(),
        P(("src", "hid"), None, None),
        P(("src", "hid")),
        P(("src", "hid")),
        P(("src", "hid")),
        P(("src", "hid"), None, None),
        P(("src", "hid")),
        P(("src", "hid")),
        P(("src", "hid")),
    )
    out_specs = (P("src", None, None, None), P())
    return jax.shard_map(body, mesh=mesh, in_specs=in_specs, out_specs=out_specs, check_vma=False)
```

profile of v0, /device:TPU:0, one launch (start us, length us, event | category | flops | bytes accessed | tf_op | source)
XLA Modules:
  0.0 277.2 jit_solution(4805491269484964007)
XLA Ops:
  7.2 0.0 all-reduce.3.cloned.1.call-start
  7.9 2.1 copy.23
  10.0 0.7 broadcast_subtract_fusion
  10.6 0.4 broadcast_in_dim.5
  11.0 8.7 %while.22 = (s32[]{:T(128)}, f32[32,196,128]{2,0,1:T(8,128)S(1)}, s32[]{:T(128)}, s32[1]{0:T(128)}, s32[32]{0:T(128)S(1)}, /*index=5*/s32[32]{0:T(128)S(1)}, f32...) while((s32[]{:T(128)}, f32[32,196,128]{2,0,1:T(8,128)S(1)}, ...), condition=%wide.region_1.2_spmd.clone, body=%wide.region_0.1_spmd.clone.sunk | while | flops 810042496 | bytes 23085684 | solution.py:58
  11.1 0.0 copy-start.1
  11.1 0.1 dynamic_slice.35
  11.2 2.1 fusion.73
  13.3 0.0 copy-done.1
  13.3 3.2 %fusion.74 = f32[16,196,128]{2,1,0:T(8,128)S(1)} fusion(f32[16,196,128]{2,0,1:T(8,128)S(1)} %fusion.73, f32[32,128,128]{2,1,0:T(8,128)S(1)} %copy-done.1, s32[]{:T(128)S(6)} %select_n.24), kind=kOutput, calls=%fused_computation.7.clone.1 | convolution fusion | flops 616562688 | bytes 4259844 | tf_op jit(solution)/shard_map/while/body/tfr,trc->tfc/dot_general | solution.py:54
  16.5 0.1 dynamic_slice.36
  16.5 0.7 fusion.75
  17.2 2.6 convolution_add_fusion.2
  19.8 0.0 copy-start.6
  19.8 0.0 copy-start.4
  19.8 0.0 copy-start.5
  19.8 1.7 copy-done
  21.5 0.0 all-reduce.3.cloned.1.call-update
  21.5 0.0 all-reduce.5.cloned.1.call-start
  22.2 0.1 mul.48
  22.3 0.0 copy-done.5
  22.3 159.6 %all-reduce.3.cloned.1.call-done = f32[32,196,128]{2,0,1:T(8,128)} async-done(((f32[32,196,128]{2,0,1:T(8,128)}), f32[32,196,128]{2,0,1:T(8,128)}) %all-reduce.3.cloned.1.call-update) | async-done | bytes 3211280 | tf_op jit(solution)/shard_map/psum | solution.py:61
  181.9 3.6 %mul.51 = f32[32,196,128]{2,0,1:T(8,128)S(1)} multiply(f32[32,196,128]{2,0,1:T(8,128)} %all-reduce.3.cloned.1.call-done, f32[32,196,128]{2,0,1:T(8,128)} %all-reduce.3.cloned.1.call-done) | non-fusion elementwise | flops 802816 | bytes 9633792 | tf_op jit(solution)/shard_map/mul | solution.py:15
  185.5 0.2 reduce_sum.21
  185.8 2.2 bitcast_multiply_fusion
  188.0 0.9 broadcast_in_dim.4
  188.9 16.7 %while.23 = (s32[]{:T(128)}, f32[8,196,128]{2,0,1:T(8,128)}, s32[]{:T(128)}, s32[1]{0:T(128)}, s32[32]{0:T(128)S(1)}, /*index=5*/s32[32]{0:T(128)S(1)}, f32[32,1...) while((s32[]{:T(128)}, f32[8,196,128]{2,0,1:T(8,128)}, ...), condition=%wide.region_5.6_spmd.clone, body=%wide.region_4.5_spmd.clone.sunk | while | flops 809440000 | bytes 20677236 | solution.py:79
  188.9 0.1 dynamic_slice.38
  189.0 1.2 fusion.82
  190.3 0.3 copy-done.2
  190.6 3.2 %fusion.83 = f32[16,196,128]{2,1,0:T(8,128)S(1)} fusion(f32[16,196,128]{2,0,1:T(8,128)S(1)} %fusion.82, f32[32,128,128]{2,1,0:T(8,128)S(1)} %copy-done.2, s32[]{:T(128)S(6)} %select_n.25), kind=kOutput, calls=%fused_computation.23.clone.1 | convolution fusion | flops 616562688 | bytes 4259844 | tf_op jit(solution)/shard_map/while/body/tfr,trc->tfc/dot_general | solution.py:74
  193.8 0.1 dynamic_slice.39
  193.8 0.7 fusion.84
  194.5 2.8 %fusion.85 = f32[8,196,128]{2,0,1:T(8,128)} fusion(f32[8,196,128]{2,0,1:T(8,128)} %get-tuple-element.375, f32[16,196,128]{2,1,0:T(8,128)S(1)} %fusion.83, s32[16]{0:T(128)S(1)} %dynamic_slice.39, pred[16]{0:T(512)(128)(4,1)S(1)} %fusion.84), kind=kOutput, calls=%fused_computation.27.clone.1 | convolution fusion | flops 38736128 | bytes 3211344 | tf_op jit(solution)/shard_map/while/body/ts,tfc->sfc/dot_general | solution.py:76
  197.3 0.1 dynamic_slice.38
  197.4 1.2 fusion.82
  198.6 0.3 copy-done.2
  199.0 3.2 %fusion.83 = f32[16,196,128]{2,1,0:T(8,128)S(1)} fusion(f32[16,196,128]{2,0,1:T(8,128)S(1)} %fusion.82, f32[32,128,128]{2,1,0:T(8,128)S(1)} %copy-done.2, s32[]{:T(128)S(6)} %select_n.25), kind=kOutput, calls=%fused_computation.23.clone.1 | convolution fusion | flops 616562688 | bytes 4259844 | tf_op jit(solution)/shard_map/while/body/tfr,trc->tfc/dot_general | solution.py:74
  202.1 0.1 dynamic_slice.39
  202.2 0.7 fusion.84
  202.9 2.8 %fusion.85 = f32[8,196,128]{2,0,1:T(8,128)} fusion(f32[8,196,128]{2,0,1:T(8,128)} %get-tuple-element.375, f32[16,196,128]{2,1,0:T(8,128)S(1)} %fusion.83, s32[16]{0:T(128)S(1)} %dynamic_slice.39, pred[16]{0:T(512)(128)(4,1)S(1)} %fusion.84), kind=kOutput, calls=%fused_computation.27.clone.1 | convolution fusion | flops 38736128 | bytes 3211344 | tf_op jit(solution)/shard_map/while/body/ts,tfc->sfc/dot_general | solution.py:76
  205.6 0.0 all-reduce.5.cloned.1.call-update
  205.7 18.3 %all-reduce.5.cloned.1.call-done = f32[8,196,128]{2,0,1:T(8,128)} async-done(((f32[8,196,128]{2,0,1:T(8,128)}), f32[8,196,128]{2,0,1:T(8,128)}) %all-reduce.5.cloned.1.call-update) | async-done | bytes 802832 | tf_op jit(solution)/shard_map/psum | solution.py:83
  224.0 2.5 multiply_reduce_fusion
  226.4 0.1 reduce_sum.27
  226.5 42.0 %psum.23 = f32[98]{0:T(128)S(1)} all-reduce(f32[98]{0:T(128)S(1)} %reduce_sum.28), channel_id=1, replica_groups=mesh['src'=16,'hid'=2] {'src'}, use_global_device_ids=true, to_apply=%region_9.10 | all-reduce | flops 98 | bytes 784 | tf_op jit(solution)/shard_map/psum | solution.py:88
  268.5 0.5 add_sqrt_fusion
  269.1 1.3 copy.24
  (11 shorter events, 0.1 us)
Async XLA Ops:
  7.2 174.7 %all-reduce.3.cloned.1.call-start = ((), (), s32[]{:S(2)}) async-start(), calls=%async_computation | async-start | bytes 6422528 | tf_op jit(solution)/shard_map/psum | solution.py:61
  11.1 2.2 copy-start.1
  19.8 1.7 copy-start
  19.8 2.4 copy-start.6
  19.8 2.5 copy-start.4
  19.8 2.5 copy-start.5
  21.5 202.4 %all-reduce.5.cloned.1.call-start = ((), (), s32[]{:S(2)}) async-start(), calls=%async_computation.1 | async-start | bytes 1605632 | tf_op jit(solution)/shard_map/psum | solution.py:83
  189.0 1.6 copy-start.2
  197.4 1.6 copy-start.2
  224.0 45.1 %copy-start.3 = (f32[8,196,128]{2,0,1:T(8,128)S(1)}, f32[8,196,128]{2,0,1:T(8,128)}, u32[]{:S(2)}) copy-start(f32[8,196,128]{2,0,1:T(8,128)} %all-reduce.5.cloned.1.call-done) | copy-start | bytes 2408452
Sparse Core Ops, SparseCore 0:
  21.6 160.2 all-reduce.2
  205.8 18.1 all-reduce.4
where the time goes:
time: 278 us; the launch traced here: 277 us
  waiting for transfers between devices  178 us (64%)
  blocking collectives  42 us (15%)
  matrix products  22.2 us (8%)
  between operations  15.5 us (6%)
  other arithmetic  11.8 us (4%)
  local copies, waits for them, and re-layouts  7.73 us (3%)
    psum x1, waiting for transfers between devices, body(): lax.psum(partial_value, 'src')  160 us
    psum x1, blocking collectives, body(): sums = lax.psum(squares, 'src')  42 us
    psum x1, waiting for transfers between devices, body(): returned = lax.psum(partial_back, 'hid')  18.3 us
    dot_general x2, matrix products, decode_group(): product = jnp.einsum('tfr,trc->tfc', blocks, tiles, precision=HIGH)  6.31 us
    dot_general x2, matrix products, decode_group(): jnp.einsum('ts,tfc->sfc', placing, product, precision=HIGH)  5.57 us
  transfers between devices with their start and end apart: 2, of which 2 were waited for; matrix products, arithmetic and copies ran while one was open for 0% of the time, Pallas kernels for 0%

commit v1 on v0

--- a/solution.py
+++ b/solution.py
@@ -85,7 +85,9 @@
     squares = jnp.sum(
         (difference * difference).reshape(src_blocks, batch, channels, width), axis=(0, 1, 3)
     )
-    sums = lax.psum(squares, "src")
+    sums = squares
+    for hop in (1, 2, 4, 8):
+        sums = sums + lax.ppermute(sums, "src", [(dev, dev ^ hop) for dev in range(16)])
     channel_rms = jnp.sqrt(sums / total_points + EPSILON)
     return (returned.reshape(source_field.shape), channel_rms)
 

time: 278 us -> 250 us (0.90)
  blocking collectives: 42 us -> 0 us
  starting transfers between devices: 0.08 us -> 8.16 us
  waiting for transfers between devices: 178 us -> 184 us
    psum x1 -> x0, blocking collectives: 42 us -> none  [body(): sums = lax.psum(squares, 'src')]
    ppermute x0 -> x4, starting transfers between devices: none -> 8.08 us  [body(): lax.ppermute(sums, 'src', [(dev, dev ^ hop) for dev in range(16)])]
    ppermute x0 -> x4, waiting for transfers between devices: none -> 5.85 us  [body(): lax.ppermute(sums, 'src', [(dev, dev ^ hop) for dev in range(16)])]
  transfers between devices with their start and end apart: 2 -> 6, of which waited for: 2 -> 6; matrix products, arithmetic and copies ran while one was open for 0% -> 1% of each run, Pallas kernels for 0% -> 0%
where the time goes in v1:
time: 250 us; the launch traced here: 249 us
  waiting for transfers between devices  184 us (74%)
  matrix products  22.2 us (9%)
  between operations  15.5 us (6%)
  other arithmetic  11.8 us (5%)
  starting transfers between devices  8.16 us (3%)
  local copies, waits for them, and re-layouts  7.72 us (3%)
    psum x1, waiting for transfers between devices, body(): lax.psum(partial_value, 'src')  159 us
    psum x1, waiting for transfers between devices, body(): returned = lax.psum(partial_back, 'hid')  18.3 us
    ppermute x4, starting transfers between devices, body(): lax.ppermute(sums, 'src', [(dev, dev ^ hop) for dev in range(16)])  8.08 us
    dot_general x2, matrix products, decode_group(): product = jnp.einsum('tfr,trc->tfc', blocks, tiles, precision=HIGH)  6.31 us
    ppermute x4, waiting for transfers between devices, body(): lax.ppermute(sums, 'src', [(dev, dev ^ hop) for dev in range(16)])  5.85 us
    dot_general x2, matrix products, decode_group(): jnp.einsum('ts,tfc->sfc', placing, product, precision=HIGH)  5.57 us
    unnamed x12, local copies, waits for them, and re-layouts  5.06 us
  transfers between devices with their start and end apart: 6, of which 6 were waited for; matrix products, arithmetic and copies ran while one was open for 1% of the time, Pallas kernels for 0%

profile of v1, /device:TPU:0, one launch (start us, length us, event | category | flops | bytes accessed | tf_op | source)
XLA Modules:
  0.0 249.1 jit_solution(4215097659516070779)
XLA Ops:
  7.2 0.0 all-reduce.3.cloned.1.call-start
  7.9 2.1 copy.23
  10.0 0.7 broadcast_subtract_fusion
  10.7 0.4 broadcast_in_dim.5
  11.1 8.7 %while.22 = (s32[]{:T(128)}, f32[32,196,128]{2,0,1:T(8,128)S(1)}, s32[]{:T(128)}, s32[1]{0:T(128)}, s32[32]{0:T(128)S(1)}, /*index=5*/s32[32]{0:T(128)S(1)}, f32...) while((s32[]{:T(128)}, f32[32,196,128]{2,0,1:T(8,128)S(1)}, ...), condition=%wide.region_1.2_spmd.clone, body=%wide.region_0.1_spmd.clone.sunk | while | flops 810042496 | bytes 23085684 | solution.py:58
  11.1 0.1 dynamic_slice.35
  11.2 2.1 fusion.73
  13.3 3.2 %fusion.74 = f32[16,196,128]{2,1,0:T(8,128)S(1)} fusion(f32[16,196,128]{2,0,1:T(8,128)S(1)} %fusion.73, f32[32,128,128]{2,1,0:T(8,128)S(1)} %copy-done.1, s32[]{:T(128)S(6)} %select_n.24), kind=kOutput, calls=%fused_computation.7.clone.1 | convolution fusion | flops 616562688 | bytes 4259844 | tf_op jit(solution)/shard_map/while/body/tfr,trc->tfc/dot_general | solution.py:54
  16.5 0.1 dynamic_slice.36
  16.5 0.7 fusion.75
  17.2 2.6 %convolution_add_fusion.2 = f32[32,196,128]{2,0,1:T(8,128)S(1)} fusion(f32[32,196,128]{2,0,1:T(8,128)S(1)} %get-tuple-element.339, f32[16,196,128]{2,1,0:T(8,128)S(1)} %fusion.74, s32[16]{0:T(128)S(1)} %dynamic_slice.36, pred[16]{0:T(512)(128)(4,1)S(1)} %fusion.75), kind=kOutput, calls=%fused_computation.6.clone.1 | convolution fusion | flops 154944512 | bytes 8028240 | tf_op jit(solution)/shard_map/while/body/th,tfc->hfc/dot_general | solution.py:55
  19.8 1.6 copy-done
  21.5 0.0 all-reduce.3.cloned.1.call-update
  21.5 0.0 all-reduce.5.cloned.1.call-start
  22.2 0.1 mul.48
  22.3 159.5 %all-reduce.3.cloned.1.call-done = f32[32,196,128]{2,0,1:T(8,128)} async-done(((f32[32,196,128]{2,0,1:T(8,128)}), f32[32,196,128]{2,0,1:T(8,128)}) %all-reduce.3.cloned.1.call-update) | async-done | bytes 3211280 | tf_op jit(solution)/shard_map/psum | solution.py:61
  181.8 3.6 %mul.51 = f32[32,196,128]{2,0,1:T(8,128)S(1)} multiply(f32[32,196,128]{2,0,1:T(8,128)} %all-reduce.3.cloned.1.call-done, f32[32,196,128]{2,0,1:T(8,128)} %all-reduce.3.cloned.1.call-done) | non-fusion elementwise | flops 802816 | bytes 9633792 | tf_op jit(solution)/shard_map/mul | solution.py:15
  185.4 0.2 reduce_sum.21
  185.7 2.2 bitcast_multiply_fusion
  187.9 0.9 broadcast_in_dim.4
  188.9 16.7 %while.23 = (s32[]{:T(128)}, f32[8,196,128]{2,0,1:T(8,128)}, s32[]{:T(128)}, s32[1]{0:T(128)}, s32[32]{0:T(128)S(1)}, /*index=5*/s32[32]{0:T(128)S(1)}, f32[32,1...) while((s32[]{:T(128)}, f32[8,196,128]{2,0,1:T(8,128)}, ...), condition=%wide.region_5.6_spmd.clone, body=%wide.region_4.5_spmd.clone.sunk | while | flops 809440000 | bytes 20677236 | solution.py:79
  188.9 0.1 dynamic_slice.38
  188.9 1.2 fusion.82
  190.2 0.3 copy-done.2
  190.5 3.2 %fusion.83 = f32[16,196,128]{2,1,0:T(8,128)S(1)} fusion(f32[16,196,128]{2,0,1:T(8,128)S(1)} %fusion.82, f32[32,128,128]{2,1,0:T(8,128)S(1)} %copy-done.2, s32[]{:T(128)S(6)} %select_n.25), kind=kOutput, calls=%fused_computation.23.clone.1 | convolution fusion | flops 616562688 | bytes 4259844 | tf_op jit(solution)/shard_map/while/body/tfr,trc->tfc/dot_general | solution.py:74
  193.7 0.1 dynamic_slice.39
  193.8 0.7 fusion.84
  194.4 2.8 %fusion.85 = f32[8,196,128]{2,0,1:T(8,128)} fusion(f32[8,196,128]{2,0,1:T(8,128)} %get-tuple-element.375, f32[16,196,128]{2,1,0:T(8,128)S(1)} %fusion.83, s32[16]{0:T(128)S(1)} %dynamic_slice.39, pred[16]{0:T(512)(128)(4,1)S(1)} %fusion.84), kind=kOutput, calls=%fused_computation.27.clone.1 | convolution fusion | flops 38736128 | bytes 3211344 | tf_op jit(solution)/shard_map/while/body/ts,tfc->sfc/dot_general | solution.py:76
  197.2 0.1 dynamic_slice.38
  197.3 1.2 fusion.82
  198.5 0.3 copy-done.2
  198.9 3.2 %fusion.83 = f32[16,196,128]{2,1,0:T(8,128)S(1)} fusion(f32[16,196,128]{2,0,1:T(8,128)S(1)} %fusion.82, f32[32,128,128]{2,1,0:T(8,128)S(1)} %copy-done.2, s32[]{:T(128)S(6)} %select_n.25), kind=kOutput, calls=%fused_computation.23.clone.1 | convolution fusion | flops 616562688 | bytes 4259844 | tf_op jit(solution)/shard_map/while/body/tfr,trc->tfc/dot_general | solution.py:74
  202.0 0.1 dynamic_slice.39
  202.1 0.7 fusion.84
  202.8 2.8 %fusion.85 = f32[8,196,128]{2,0,1:T(8,128)} fusion(f32[8,196,128]{2,0,1:T(8,128)} %get-tuple-element.375, f32[16,196,128]{2,1,0:T(8,128)S(1)} %fusion.83, s32[16]{0:T(128)S(1)} %dynamic_slice.39, pred[16]{0:T(512)(128)(4,1)S(1)} %fusion.84), kind=kOutput, calls=%fused_computation.27.clone.1 | convolution fusion | flops 38736128 | bytes 3211344 | tf_op jit(solution)/shard_map/while/body/ts,tfc->sfc/dot_general | solution.py:76
  205.6 18.3 %all-reduce.5.cloned.1.call-done = f32[8,196,128]{2,0,1:T(8,128)} async-done(((f32[8,196,128]{2,0,1:T(8,128)}), f32[8,196,128]{2,0,1:T(8,128)}) %all-reduce.5.cloned.1.call-update) | async-done | bytes 802832 | tf_op jit(solution)/shard_map/psum | solution.py:83
  223.9 2.5 multiply_reduce_fusion
  226.4 0.1 reduce_sum.27
  226.5 1.8 collective-permute-start
  228.3 1.8 collective-permute-done
  230.1 1.8 collective-permute-start.1
  231.9 1.8 collective-permute-done.1
  233.7 1.8 collective-permute-start.2
  235.4 1.8 collective-permute-done.2
  237.2 2.7 %collective-permute-start.3 = (f32[98]{0:T(128)S(1)}, f32[98]{0:T(128)S(1)}, u32[]{:S(2)}, u32[]{:S(2)}) collective-permute-start(f32[98]{0:T(128)S(1)} %add.91), channel_id=1, source_target_pairs={{0,16},{2,18},{4,20},{6,22},{8,24},{10,26},{12,28},{14,30},{16,0},... | collective-permute-start | bytes 1184 | tf_op jit(solution)/shard_map/ppermute | solution.py:90
  239.9 1.3 copy.24
  241.2 0.5 collective-permute-done.3
  241.7 0.5 add_sqrt_fusion
  (21 shorter events, 0.1 us)
Async XLA Ops:
  7.2 174.6 %all-reduce.3.cloned.1.call-start = ((), (), s32[]{:S(2)}) async-start(), calls=%async_computation | async-start | bytes 6422528 | tf_op jit(solution)/shard_map/psum | solution.py:61
  11.1 2.2 copy-start.1
  19.8 1.7 copy-start
  19.8 2.4 copy-start.6
  19.8 2.5 %copy-start.4 = (s32[32]{0:T(128)S(1)}, s32[32]{0:T(128)}, u32[]{:S(2)}) copy-start(s32[32]{0:T(128)} %param.22) | copy-start | bytes 388
  19.8 2.5 copy-start.5
  21.5 202.4 %all-reduce.5.cloned.1.call-start = ((), (), s32[]{:S(2)}) async-start(), calls=%async_computation.1 | async-start | bytes 1605632 | tf_op jit(solution)/shard_map/psum | solution.py:83
  188.9 1.6 copy-start.2
  197.3 1.6 copy-start.2
  223.9 16.1 %copy-start.3 = (f32[8,196,128]{2,0,1:T(8,128)S(1)}, f32[8,196,128]{2,0,1:T(8,128)}, u32[]{:S(2)}) copy-start(f32[8,196,128]{2,0,1:T(8,128)} %all-reduce.5.cloned.1.call-done) | copy-start | bytes 2408452
  226.5 3.6 %collective-permute-start = (f32[98]{0:T(128)S(1)}, f32[98]{0:T(128)S(1)}, u32[]{:S(2)}, u32[]{:S(2)}) collective-permute-start(f32[98]{0:T(128)S(1)} %reduce_sum.28), channel_id=1, source_target_pairs={{0,2},{2,0},{4,6},{6,4},{8,10},{10,8},{12,14},{14,12},{16,18},{18,... | collective-permute-start | bytes 1184 | tf_op jit(solution)/shard_map/ppermute | solution.py:90
  230.1 3.6 %collective-permute-start.1 = (f32[98]{0:T(128)S(1)}, f32[98]{0:T(128)S(1)}, u32[]{:S(2)}, u32[]{:S(2)}) collective-permute-start(f32[98]{0:T(128)S(1)} %add.89), channel_id=1, source_target_pairs={{0,4},{2,6},{4,0},{6,2},{8,12},{10,14},{12,8},{14,10},{16,20},{18,... | collective-permute-start | bytes 1184 | tf_op jit(solution)/shard_map/ppermute | solution.py:90
  233.7 3.6 %collective-permute-start.2 = (f32[98]{0:T(128)S(1)}, f32[98]{0:T(128)S(1)}, u32[]{:S(2)}, u32[]{:S(2)}) collective-permute-start(f32[98]{0:T(128)S(1)} %add.90), channel_id=1, source_target_pairs={{0,8},{2,10},{4,12},{6,14},{8,0},{10,2},{12,4},{14,6},{16,24},{18,... | collective-permute-start | bytes 1184 | tf_op jit(solution)/shard_map/ppermute | solution.py:90
  237.2 4.5 %collective-permute-start.3 = (f32[98]{0:T(128)S(1)}, f32[98]{0:T(128)S(1)}, u32[]{:S(2)}, u32[]{:S(2)}) collective-permute-start(f32[98]{0:T(128)S(1)} %add.91), channel_id=1, source_target_pairs={{0,16},{2,18},{4,20},{6,22},{8,24},{10,26},{12,28},{14,30},{16,0},... | collective-permute-start | bytes 1184 | tf_op jit(solution)/shard_map/ppermute | solution.py:90
Sparse Core Ops, SparseCore 0:
  21.6 160.1 all-reduce.2
  205.7 18.1 all-reduce.4
